TPU v7x, 32 devices: a whole 2x2x4 slice. The times are simulated.
32 devices in a mesh: cluster: 4 (over y, x), member: 8 (over z, core).
Axes of the slice: x: 2, y: 2, z: 4, core: 2. Of those that a mesh axis runs over, the one named last changes fastest.
Arguments:
- embeddings: bfloat16 [8192, 4096], P(('cluster', 'member')), may hold values from -15 to 15, as said below
- start_basis: bfloat16 [4096, 512], P(('cluster', 'member')), may hold values from -6 to 6
- cluster_ids: int32 [8192], P(('cluster', 'member')), may hold values from 0 to 7
- valid_counts: int32 [4], P('cluster'), may hold values from 512 to 2048
Outputs:
- subspace: float32 [4096, 512], P(('cluster', 'member'))
- nearest: float32 [8192], P(('cluster', 'member'))
Inputs may be any that keep to these rules, and one draw needn't show every extreme that they name: `embeddings`: Real-valued entries.
All inputs are finite; a program needn't handle non-finite values.
Results may differ from a plain program's by a relative error of at most 0.0042.
Values may be sent and summed in bfloat16 or wider, within the bound.
No kernel may reach another device: no remote copies, remote signals or barrier semaphores. Data moves between devices by JAX's collectives and lax.ppermute only.
A program may use at most 64 MiB of HBM per device.

v0:
```python
import math
import jax
import jax.numpy as jnp
from jax import lax
from jax.sharding import PartitionSpec as P

D = 4096
ITERS = 2
EPS = 1e-06


def spread_basis(local_rows):
    return lax.all_gather(local_rows, ("cluster", "member"), axis=0, tiled=True)


def reduce_image(centered, projected):
    return lax.psum_scatter(
        lax.dot_general(
            centered, projected, (((0,), (0,)), ((), ())), preferred_element_type=jnp.float32
        ),
        ("cluster", "member"),
        scatter_dimension=0,
        tiled=True,
    )


def body(embeddings, start_basis, cluster_ids, valid_counts):
    row_count = embeddings.shape[0]
    total_rows = row_count * lax.axis_size(("cluster", "member"))
    ones_row = jnp.ones((1, row_count), jnp.bfloat16)
    column_sums = jnp.dot(ones_row, embeddings, preferred_element_type=jnp.float32)[0]
    average = lax.psum(column_sums, ("cluster", "member")) / total_rows
    centered = (embeddings.astype(jnp.float32) - average).astype(jnp.bfloat16)
    basis_full = spread_basis(start_basis)
    orthonormal = None
    for sweep in range(ITERS):
        projected = jnp.dot(centered, basis_full, preferred_element_type=jnp.float32).astype(
            jnp.bfloat16
        )
        image = reduce_image(centered, projected) / total_rows
        local_gram = jnp.dot(image.T, image, precision=lax.Precision.HIGHEST)
        gram = lax.psum(local_gram, ("cluster", "member"))
        lower = jnp.linalg.cholesky(gram)
        orthonormal = jax.scipy.linalg.solve_triangular(lower, image.T, lower=True).T
        basis_full = spread_basis(orthonormal.astype(jnp.bfloat16))
    subspace = orthonormal * math.sqrt(D)
    coords = jnp.dot(centered, basis_full, preferred_element_type=jnp.float32)
    unit = (coords * lax.rsqrt(jnp.sum(coords * coords, axis=1, keepdims=True) + EPS)).astype(
        jnp.bfloat16
    )
    label_values = cluster_ids.astype(jnp.bfloat16)
    limit = valid_counts[0]
    own_index = lax.axis_index("member") * row_count + jnp.arange(row_count, dtype=jnp.int32)
    initial = jnp.full((row_count,), -1.0, jnp.float32)
    piece_units = lax.all_gather(unit, "member", axis=0, tiled=True)
    piece_labels = lax.all_gather(label_values, "member", axis=0, tiled=True)
    scores = lax.dot_general(
        unit, piece_units, (((1,), (1,)), ((), ())), preferred_element_type=jnp.float32
    )
    others = jnp.arange(piece_units.shape[0], dtype=jnp.int32)
    allowed = (
        (label_values[:, None] == piece_labels[None, :])
        & (others[None, :] < limit)
        & (others[None, :] != own_index[:, None])
    )
    nearest = jnp.maximum(initial, jnp.max(jnp.where(allowed, scores, -1.0), axis=1))
    return (subspace, nearest)


def solution(mesh):
    placed = (
        P(("cluster", "member"), None),
        P(("cluster", "member"), None),
        P(("cluster", "member")),
        P("cluster"),
    )
    return jax.shard_map(
        body,
        mesh=mesh,
        in_specs=placed,
        out_specs=(P(("cluster", "member"), None), P(("cluster", "member"))),
        check_vma=False,
    )
```

profile of v0, /device:TPU:0, one launch (start us, length us, event | category | flops | bytes accessed | tf_op | source)
XLA Modules:
  0.0 1155.7 jit_solution(3383755361846079378)
XLA Ops:
  9.9 42.8 %psum.21 = f32[4096]{0:T(1024)S(1)} all-reduce(f32[4096]{0:T(1024)S(1)} %bitcast.117), channel_id=1, replica_groups=mesh['cluster'=4,'member'=8] {'cluster','member'}, use_global_device_ids=true, to_apply=%region_0.0 | all-reduce | flops 4096 | bytes 32768 | tf_op jit(solution)/shard_map/psum | solution.py:32
  52.8 22.7 %all-gather.6.cloned.1.call-done = bf16[4096,512]{1,0:T(8,128)(2,1)} async-done(((bf16[128,512]{1,0:T(8,128)(2,1)}), bf16[4096,512]{1,0:T(8,128)(2,1)}) %all-gather.6.cloned.1.call-update) | async-done | bytes 4194320 | tf_op jit(solution)/shard_map/all_gather | solution.py:13
  83.4 153.1 %reduce-scatter.3.cloned.1.call-done = f32[128,512]{1,0:T(8,128)} async-done(((f32[4096,512]{1,0:T(8,128)}), f32[128,512]{1,0:T(8,128)}) %reduce-scatter.3.cloned.1.call-update) | async-done | bytes 262160 | tf_op jit(solution)/shard_map/reduce_scatter | solution.py:17
  240.5 129.6 %all-reduce.4.cloned.1.call-done = f32[512,512]{0,1:T(8,128)} async-done(((f32[512,512]{0,1:T(8,128)}), f32[512,512]{0,1:T(8,128)}) %all-reduce.4.cloned.1.call-update) | async-done | bytes 1048592 | tf_op jit(solution)/shard_map/psum | solution.py:42
  375.3 11.7 %cholesky.286 = f32[128,128]{1,0:T(8,128)S(1)} custom-call(f32[128,128]{1,0:T(8,128)S(1)} %cholesky.426), custom_call_target="Cholesky" | custom-call | tf_op jit(solution)/shard_map/jit(cholesky)/cholesky | solution.py:43
  400.7 11.7 %cholesky.305 = f32[128,128]{1,0:T(8,128)S(1)} custom-call(f32[128,128]{1,0:T(8,128)S(1)} %cholesky.430), custom_call_target="Cholesky" | custom-call | tf_op jit(solution)/shard_map/jit(cholesky)/cholesky | solution.py:43
  412.9 10.3 custom-call.28
  426.3 13.2 %cholesky.326 = f32[128,128]{1,0:T(8,128)} custom-call(f32[128,128]{1,0:T(8,128)} %cholesky.435), custom_call_target="Cholesky" | custom-call | tf_op jit(solution)/shard_map/jit(cholesky)/cholesky | solution.py:43
  441.6 11.3 custom-call.29
  455.1 11.7 %cholesky.343 = f32[128,128]{1,0:T(8,128)S(1)} custom-call(f32[128,128]{1,0:T(8,128)S(1)} %convolution_subtract_fusion.11), custom_call_target="Cholesky" | custom-call | tf_op jit(solution)/shard_map/jit(cholesky)/cholesky | solution.py:43
  472.6 12.0 %while.4 = (s32[]{:T(128)}, f32[512,512]{1,0:T(8,128)}, s32[4,2]{0,1:T(2,128)S(1)}, f32[4,128,128]{2,1,0:T(8,128)S(1)}, s32[]{:T(128)}) while((s32[]{:T(128)}, f32[512,512]{1,0:T(8,128)}, s32[4,2]{0,1:T(2,128)S(1)}, f32[4,128,128]{2,1,0:T(8,128)S(1)}, s32[]{:T(128)}) %tuple.59), condition=%wide.while_cond, body=%wide.while_body.sunk | while | flops 2 | bytes 131181 | solution.py:44
  485.2 39.3 %custom-call.30 = f32[4,128,128]{1,2,0:T(8,128)S(1)} custom-call(f32[4,128,128]{2,1,0:T(8,128)S(1)} %get-tuple-element.18), custom_call_target="InvertDiagBlocksLowerTriangular" | custom-call | tf_op jit(solution)/shard_map/jit(_solve_triangular)/triangular_solve | solution.py:44
  530.3 64.1 %all-gather.8.cloned.1.call-done = bf16[4096,512]{0,1:T(8,128)(2,1)} async-done(((bf16[128,512]{0,1:T(8,128)(2,1)}), bf16[4096,512]{0,1:T(8,128)(2,1)}) %all-gather.8.cloned.1.call-update) | async-done | bytes 4194320 | tf_op jit(solution)/shard_map/all_gather | solution.py:13
  602.5 152.4 %reduce-scatter.5.cloned.1.call-done = f32[128,512]{1,0:T(8,128)} async-done(((f32[4096,512]{1,0:T(8,128)}), f32[128,512]{1,0:T(8,128)}) %reduce-scatter.5.cloned.1.call-update) | async-done | bytes 262160 | tf_op jit(solution)/shard_map/reduce_scatter | solution.py:17
  758.4 130.1 %all-reduce.6.cloned.1.call-done = f32[512,512]{0,1:T(8,128)} async-done(((f32[512,512]{0,1:T(8,128)}), f32[512,512]{0,1:T(8,128)}) %all-reduce.6.cloned.1.call-update) | async-done | bytes 1048592 | tf_op jit(solution)/shard_map/psum | solution.py:42
  893.6 11.7 %cholesky.358 = f32[128,128]{1,0:T(8,128)S(1)} custom-call(f32[128,128]{1,0:T(8,128)S(1)} %cholesky.439), custom_call_target="Cholesky" | custom-call | tf_op jit(solution)/shard_map/jit(cholesky)/cholesky | solution.py:43
  919.1 11.7 %cholesky.377 = f32[128,128]{1,0:T(8,128)S(1)} custom-call(f32[128,128]{1,0:T(8,128)S(1)} %cholesky.443), custom_call_target="Cholesky" | custom-call | tf_op jit(solution)/shard_map/jit(cholesky)/cholesky | solution.py:43
  946.1 13.2 %cholesky.398 = f32[128,128]{1,0:T(8,128)} custom-call(f32[128,128]{1,0:T(8,128)} %cholesky.448), custom_call_target="Cholesky" | custom-call | tf_op jit(solution)/shard_map/jit(cholesky)/cholesky | solution.py:43
  961.5 11.3 custom-call.33
  975.0 12.3 %cholesky.415 = f32[128,128]{1,0:T(8,128)} custom-call(f32[128,128]{1,0:T(8,128)S(1)} %convolution_subtract_fusion.9), custom_call_target="Cholesky" | custom-call | tf_op jit(solution)/shard_map/jit(cholesky)/cholesky | solution.py:43
  992.7 11.6 %while.5 = (s32[]{:T(128)}, f32[512,512]{1,0:T(8,128)}, s32[4,2]{0,1:T(2,128)S(1)}, f32[4,128,128]{2,1,0:T(8,128)S(1)}, s32[]{:T(128)}) while((s32[]{:T(128)}, f32[512,512]{1,0:T(8,128)}, s32[4,2]{0,1:T(2,128)S(1)}, f32[4,128,128]{2,1,0:T(8,128)S(1)}, s32[]{:T(128)}) %tuple.81), condition=%wide.while_cond.clone, body=%wide.while_body.clone.sunk | while | flops 2 | bytes 131181 | solution.py:44
  1004.3 39.3 %custom-call.34 = f32[4,128,128]{1,2,0:T(8,128)S(1)} custom-call(f32[4,128,128]{2,1,0:T(8,128)S(1)} %get-tuple-element.19), custom_call_target="InvertDiagBlocksLowerTriangular" | custom-call | tf_op jit(solution)/shard_map/jit(_solve_triangular)/triangular_solve | solution.py:44
  1049.4 64.1 %all-gather.10.cloned.1.call-done = bf16[4096,512]{0,1:T(8,128)(2,1)} async-done(((bf16[128,512]{0,1:T(8,128)(2,1)}), bf16[4096,512]{0,1:T(8,128)(2,1)}) %all-gather.10.cloned.1.call-update) | async-done | bytes 4194320 | tf_op jit(solution)/shard_map/all_gather | solution.py:13
  1129.4 16.0 %all-gather.12.cloned.1.call-done = bf16[2048,512]{1,0:T(8,128)(2,1)} async-done(((bf16[256,512]{1,0:T(8,128)(2,1)}), bf16[2048,512]{1,0:T(8,128)(2,1)}) %all-gather.12.cloned.1.call-update) | async-done | bytes 2097168 | tf_op jit(solution)/shard_map/all_gather | solution.py:55
  (152 shorter events, 151.3 us)
Async XLA Ops:
  7.2 68.3 %copy-start = (bf16[256,4096]{1,0:T(8,128)(2,1)S(1)}, bf16[256,4096]{1,0:T(8,128)(2,1)}, u32[]{:S(2)}) copy-start(bf16[256,4096]{1,0:T(8,128)(2,1)} %param.7) | copy-start | bytes 6291460
  7.2 68.3 %all-gather.6.cloned.1.call-start = ((), (), s32[]{:S(2)}) async-start(), calls=%async_computation.2 | async-start | bytes 4325376 | tf_op jit(solution)/shard_map/all_gather | solution.py:13
  7.9 228.5 %reduce-scatter.3.cloned.1.call-start = ((), (), s32[]{:S(2)}) async-start(), calls=%async_computation.3 | async-start | bytes 8650752 | tf_op jit(solution)/shard_map/reduce_scatter | solution.py:17
  83.3 286.8 %all-reduce.4.cloned.1.call-start = ((), (), s32[]{:S(2)}) async-start(), calls=%async_computation.4 | async-start | bytes 2097152 | tf_op jit(solution)/shard_map/psum | solution.py:42
  236.4 4.1 copy-start.5
  239.6 354.8 %all-gather.8.cloned.1.call-start = ((), (), s32[]{:S(2)}) async-start(), calls=%async_computation.5 | async-start | bytes 4325376 | tf_op jit(solution)/shard_map/all_gather | solution.py:13
  370.1 2.7 copy-start.1
  374.3 1.0 copy-start.4
  400.0 0.7 copy-start.8
  466.8 5.8 copy-start.12
  484.7 0.6 copy-start.9
  530.3 224.6 %reduce-scatter.5.cloned.1.call-start = ((), (), s32[]{:S(2)}) async-start(), calls=%async_computation.6 | async-start | bytes 8650752 | tf_op jit(solution)/shard_map/reduce_scatter | solution.py:17
  602.4 286.0 %all-reduce.6.cloned.1.call-start = ((), (), s32[]{:S(2)}) async-start(), calls=%async_computation.7 | async-start | bytes 2097152 | tf_op jit(solution)/shard_map/psum | solution.py:42
  754.9 3.5 copy-start.6
  758.1 355.5 %all-gather.10.cloned.1.call-start = ((), (), s32[]{:S(2)}) async-start(), calls=%async_computation.8 | async-start | bytes 4325376 | tf_op jit(solution)/shard_map/all_gather | solution.py:13
  888.5 2.7 copy-start.2
  892.6 1.0 copy-start.3
  918.4 0.7 copy-start.7
  973.8 18.9 %copy-start.10 = (s32[4,2]{0,1:T(2,128)S(1)}, s32[4,2]{0,1:T(2,128)}, u32[]{:S(2)}) copy-start(s32[4,2]{0,1:T(2,128)} %copy-done.9) | copy-start | bytes 100
  1049.3 68.6 %copy-start.11 = (s32[256]{0:T(256)S(1)}, s32[256]{0:T(256)}, u32[]{:S(2)}) copy-start(s32[256]{0:T(256)} %param.9) | copy-start | bytes 3076
  1049.3 96.1 %all-gather.12.cloned.1.call-start = ((), (), s32[]{:S(2)}) async-start(), calls=%async_computation.9 | async-start | bytes 2359296 | tf_op jit(solution)/shard_map/all_gather | solution.py:55
Sparse Core Ops, SparseCore 0:
  11.0 64.3 all-gather.5
  83.5 152.9 reduce-scatter.2
  241.6 128.4 all-reduce.3
  530.4 64.0 all-gather.7
  602.5 152.2 reduce-scatter.4
  759.9 128.4 all-reduce.5
  1049.4 64.0 all-gather.9
  1118.1 27.3 all-gather.11
where the time goes:
time: 1160 us
  waiting for transfers between devices  733 us (63%)
  other arithmetic  259 us (22%)
  matrix products  54.7 us (5%)
  blocking collectives  52.6 us (5%)
  local copies, waits for them, and re-layouts  35.1 us (3%)
  between operations  20.6 us (2%)
    reduce_scatter x2, waiting for transfers between devices, reduce_image(): lax.psum_scatter(lax.dot_general(centered, projected, (((0,), (0,)), ((),...  305 us
    psum x2, waiting for transfers between devices, body(): gram = lax.psum(local_gram, ('cluster', 'member'))  260 us
    another operation x29, other arithmetic, body(): lower = jnp.linalg.cholesky(gram)  172 us
    all_gather x3, waiting for transfers between devices, spread_basis(): return lax.all_gather(local_rows, ('cluster', 'member'), axis=0, tiled=True)  151 us
    another operation x5, other arithmetic, body(): jax.scipy.linalg.solve_triangular(lower, image.T, lower=True)  81.4 us
    psum x1, blocking collectives, body(): average = lax.psum(column_sums, ('cluster', 'member')) / total_rows  42.8 us
    another operation x27, local copies, waits for them, and re-layouts, body(): jax.scipy.linalg.solve_triangular(lower, image.T, lower=True)  23.5 us
  transfers between devices with their start and end apart: 8, of which 8 were waited for; matrix products, arithmetic and copies ran while one was open for 0% of the time, Pallas kernels for 0%

commit v1 on v0

--- a/solution.py
+++ b/solution.py
@@ -39,7 +39,7 @@
         )
         image = reduce_image(centered, projected) / total_rows
         local_gram = jnp.dot(image.T, image, precision=lax.Precision.HIGHEST)
-        gram = lax.psum(local_gram, ("cluster", "member"))
+        gram = jnp.sum(lax.all_gather(local_gram, ("cluster", "member")), axis=0)
         lower = jnp.linalg.cholesky(gram)
         orthonormal = jax.scipy.linalg.solve_triangular(lower, image.T, lower=True).T
         basis_full = spread_basis(orthonormal.astype(jnp.bfloat16))

time: 1160 us -> 1310 us (1.13)
  waiting for transfers between devices: 733 us -> 853 us
  other arithmetic: 259 us -> 284 us
    all_gather x0 -> x2, waiting for transfers between devices: none -> 382 us  [body(): gram = jnp.sum(lax.all_gather(local_gram, ('cluster', 'member')), axis=0)]
    psum x2 -> x0, waiting for transfers between devices: 260 us -> none  [body(): gram = lax.psum(local_gram, ('cluster', 'member'))]
    reduce_sum x0 -> x2, other arithmetic: none -> 25.4 us  [body(): gram = jnp.sum(lax.all_gather(local_gram, ('cluster', 'member')), axis=0)]
where the time goes in v1:
time: 1310 us; the launch traced here: 1300 us
  waiting for transfers between devices  853 us (65%)
  other arithmetic  284 us (22%)
  matrix products  54.5 us (4%)
  blocking collectives  52.7 us (4%)
  local copies, waits for them, and re-layouts  36.2 us (3%)
  between operations  20.5 us (2%)
    all_gather x2, waiting for transfers between devices, body(): gram = jnp.sum(lax.all_gather(local_gram, ('cluster', 'member')), axis=0)  382 us
    reduce_scatter x2, waiting for transfers between devices, reduce_image(): lax.psum_scatter(lax.dot_general(centered, projected, (((0,), (0,)), ((),...  305 us
    another operation x29, other arithmetic, body(): lower = jnp.linalg.cholesky(gram)  170 us
    all_gather x3, waiting for transfers between devices, spread_basis(): return lax.all_gather(local_rows, ('cluster', 'member'), axis=0, tiled=True)  149 us
    another operation x5, other arithmetic, body(): jax.scipy.linalg.solve_triangular(lower, image.T, lower=True)  81.8 us
    psum x1, blocking collectives, body(): average = lax.psum(column_sums, ('cluster', 'member')) / total_rows  42.8 us
    another operation x27, local copies, waits for them, and re-layouts, body(): jax.scipy.linalg.solve_triangular(lower, image.T, lower=True)  27.3 us
  transfers between devices with their start and end apart: 8, of which 8 were waited for; matrix products, arithmetic and copies ran while one was open for 0% of the time, Pallas kernels for 0%

profile of v1, /device:TPU:0, one launch (start us, length us, event | category | flops | bytes accessed | tf_op | source)
XLA Modules:
  0.0 1301.4 jit_solution(2009084249995780442)
XLA Ops:
  9.9 42.8 %psum.7 = f32[4096]{0:T(1024)S(1)} all-reduce(f32[4096]{0:T(1024)S(1)} %bitcast.121), channel_id=1, replica_groups=mesh['cluster'=4,'member'=8] {'cluster','member'}, use_global_device_ids=true, to_apply=%region_0.0 | all-reduce | flops 4096 | bytes 32768 | tf_op jit(solution)/shard_map/psum | solution.py:32
  52.8 22.7 %all-gather.10.cloned.1.call-done = bf16[4096,512]{1,0:T(8,128)(2,1)} async-done(((bf16[128,512]{1,0:T(8,128)(2,1)}), bf16[4096,512]{1,0:T(8,128)(2,1)}) %all-gather.10.cloned.1.call-update) | async-done | bytes 4194320 | tf_op jit(solution)/shard_map/all_gather | solution.py:13
  83.4 152.3 %reduce-scatter.3.cloned.1.call-done = f32[128,512]{1,0:T(8,128)} async-done(((f32[4096,512]{1,0:T(8,128)}), f32[128,512]{1,0:T(8,128)}) %reduce-scatter.3.cloned.1.call-update) | async-done | bytes 262160 | tf_op jit(solution)/shard_map/reduce_scatter | solution.py:17
  240.3 190.7 %all-gather.18.cloned.1.call-done = f32[16384,512]{1,0:T(8,128)} async-done(((f32[512,512]{1,0:T(8,128)}), f32[16384,512]{1,0:T(8,128)}) %all-gather.18.cloned.1.call-update) | async-done | bytes 33554448 | tf_op jit(solution)/shard_map/all_gather | solution.py:42
  431.0 12.7 reduce_sum.27
  447.5 11.7 cholesky.286
  472.9 11.7 cholesky.305
  498.3 13.2 %cholesky.326 = f32[128,128]{1,0:T(8,128)} custom-call(f32[128,128]{1,0:T(8,128)} %cholesky.435), custom_call_target="Cholesky" | custom-call | tf_op jit(solution)/shard_map/jit(cholesky)/cholesky | solution.py:43
  513.6 11.3 custom-call.29
  527.2 11.7 cholesky.343
  545.4 12.0 while.4
  558.0 39.3 %custom-call.30 = f32[4,128,128]{1,2,0:T(8,128)S(1)} custom-call(f32[4,128,128]{2,1,0:T(8,128)S(1)} %get-tuple-element.18), custom_call_target="InvertDiagBlocksLowerTriangular" | custom-call | tf_op jit(solution)/shard_map/jit(_solve_triangular)/triangular_solve | solution.py:44
  603.1 63.4 %all-gather.12.cloned.1.call-done = bf16[4096,512]{0,1:T(8,128)(2,1)} async-done(((bf16[128,512]{0,1:T(8,128)(2,1)}), bf16[4096,512]{0,1:T(8,128)(2,1)}) %all-gather.12.cloned.1.call-update) | async-done | bytes 4194320 | tf_op jit(solution)/shard_map/all_gather | solution.py:13
  674.5 152.6 %reduce-scatter.5.cloned.1.call-done = f32[128,512]{1,0:T(8,128)} async-done(((f32[4096,512]{1,0:T(8,128)}), f32[128,512]{1,0:T(8,128)}) %reduce-scatter.5.cloned.1.call-update) | async-done | bytes 262160 | tf_op jit(solution)/shard_map/reduce_scatter | solution.py:17
  831.2 190.9 %all-gather.20.cloned.1.call-done = f32[16384,512]{1,0:T(8,128)} async-done(((f32[512,512]{1,0:T(8,128)}), f32[16384,512]{1,0:T(8,128)}) %all-gather.20.cloned.1.call-update) | async-done | bytes 33554448 | tf_op jit(solution)/shard_map/all_gather | solution.py:42
  1022.1 12.7 reduce_sum.28
  1038.5 11.7 cholesky.358
  1064.0 11.7 cholesky.377
  1090.8 13.2 %cholesky.398 = f32[128,128]{1,0:T(8,128)} custom-call(f32[128,128]{1,0:T(8,128)} %cholesky.448), custom_call_target="Cholesky" | custom-call | tf_op jit(solution)/shard_map/jit(cholesky)/cholesky | solution.py:43
  1119.7 11.7 cholesky.415
  1136.0 14.8 %while.5 = (s32[]{:T(128)}, f32[512,512]{1,0:T(8,128)}, s32[4,2]{0,1:T(2,128)}, f32[4,128,128]{2,1,0:T(8,128)S(1)}, s32[]{:T(128)}) while((s32[]{:T(128)}, f32[512,512]{1,0:T(8,128)}, s32[4,2]{0,1:T(2,128)}, f32[4,128,128]{2,1,0:T(8,128)S(1)}, s32[]{:T(128)}) %tuple.81), condition=%wide.while_cond.clone, body=%wide.while_body.clone.sunk | while | flops 2 | bytes 131181 | solution.py:44
  1150.7 39.3 %custom-call.34 = f32[4,128,128]{1,2,0:T(8,128)S(1)} custom-call(f32[4,128,128]{2,1,0:T(8,128)S(1)} %get-tuple-element.19), custom_call_target="InvertDiagBlocksLowerTriangular" | custom-call | tf_op jit(solution)/shard_map/jit(_solve_triangular)/triangular_solve | solution.py:44
  1195.8 63.4 %all-gather.14.cloned.1.call-done = bf16[4096,512]{0,1:T(8,128)(2,1)} async-done(((bf16[128,512]{0,1:T(8,128)(2,1)}), bf16[4096,512]{0,1:T(8,128)(2,1)}) %all-gather.14.cloned.1.call-update) | async-done | bytes 4194320 | tf_op jit(solution)/shard_map/all_gather | solution.py:13
  1275.1 16.0 %all-gather.16.cloned.1.call-done = bf16[2048,512]{1,0:T(8,128)(2,1)} async-done(((bf16[256,512]{1,0:T(8,128)(2,1)}), bf16[2048,512]{1,0:T(8,128)(2,1)}) %all-gather.16.cloned.1.call-update) | async-done | bytes 2097168 | tf_op jit(solution)/shard_map/all_gather | solution.py:55
  (142 shorter events, 174.1 us)
Async XLA Ops:
  7.2 68.3 %copy-start = (bf16[256,4096]{1,0:T(8,128)(2,1)S(1)}, bf16[256,4096]{1,0:T(8,128)(2,1)}, u32[]{:S(2)}) copy-start(bf16[256,4096]{1,0:T(8,128)(2,1)} %param.7) | copy-start | bytes 6291460
  7.2 68.3 %all-gather.10.cloned.1.call-start = ((), (), s32[]{:S(2)}) async-start(), calls=%async_computation.2 | async-start | bytes 4325376 | tf_op jit(solution)/shard_map/all_gather | solution.py:13
  7.9 227.8 %reduce-scatter.3.cloned.1.call-start = ((), (), s32[]{:S(2)}) async-start(), calls=%async_computation.3 | async-start | bytes 8650752 | tf_op jit(solution)/shard_map/reduce_scatter | solution.py:17
  83.3 347.7 %all-gather.18.cloned.1.call-start = ((), (), s32[]{:S(2)}) async-start(), calls=%async_computation.8 | async-start | bytes 34603008 | tf_op jit(solution)/shard_map/all_gather | solution.py:42
  238.8 427.7 %all-gather.12.cloned.1.call-start = ((), (), s32[]{:S(2)}) async-start(), calls=%async_computation.4 | async-start | bytes 4325376 | tf_op jit(solution)/shard_map/all_gather | solution.py:13
  446.5 1.0 copy-start.2
  472.2 0.7 copy-start.4
  557.5 0.6 copy-start.5
  603.1 224.0 %reduce-scatter.5.cloned.1.call-start = ((), (), s32[]{:S(2)}) async-start(), calls=%async_computation.5 | async-start | bytes 8650752 | tf_op jit(solution)/shard_map/reduce_scatter | solution.py:17
  674.4 347.6 %all-gather.20.cloned.1.call-start = ((), (), s32[]{:S(2)}) async-start(), calls=%async_computation.9 | async-start | bytes 34603008 | tf_op jit(solution)/shard_map/all_gather | solution.py:42
  830.2 429.0 %all-gather.14.cloned.1.call-start = ((), (), s32[]{:S(2)}) async-start(), calls=%async_computation.6 | async-start | bytes 4325376 | tf_op jit(solution)/shard_map/all_gather | solution.py:13
  1037.5 1.0 copy-start.1
  1063.3 0.7 copy-start.3
  1195.8 67.9 %copy-start.6 = (s32[256]{0:T(256)S(1)}, s32[256]{0:T(256)}, u32[]{:S(2)}) copy-start(s32[256]{0:T(256)} %param.9) | copy-start | bytes 3076
  1195.8 95.3 %all-gather.16.cloned.1.call-start = ((), (), s32[]{:S(2)}) async-start(), calls=%async_computation.7 | async-start | bytes 2359296 | tf_op jit(solution)/shard_map/all_gather | solution.py:55
Sparse Core Ops, SparseCore 0:
  11.0 64.3 all-gather.9
  83.5 152.1 reduce-scatter.2
  238.9 192.0 all-gather.17
  603.2 63.2 all-gather.11
  674.6 152.4 reduce-scatter.4
  830.3 191.7 all-gather.19
  1195.9 63.2 all-gather.13
  1263.7 27.3 all-gather.15
